TPU v7x, 32 devices: a whole 2x2x4 slice. The times are simulated.
32 devices in a mesh: expert: 8 (over z, core), mp: 4 (over y, x).
Axes of the slice: x: 2, y: 2, z: 4, core: 2. Of those that a mesh axis runs over, the one named last changes fastest.
Arguments:
- tokens: bfloat16 [2, 2560, 2048], P(None, 'expert', 'mp'), may hold values from -6 to 6
- expert_index: int32 [2, 2560], P(None, 'expert'), may hold values from 0 to 7
- slot_index: int32 [2, 2560], P(None, 'expert'), may hold values from 0 to 5, as said below
- kept_mask: int32 [2, 2560], P(None, 'expert'), may hold values from 0 to 1
- gate_prob: float32 [2, 2560], P(None, 'expert'), may hold values from 0.2 to 1
- w_in: bfloat16 [8, 2048, 6144], P('expert', None, 'mp'), may hold values from -0.125 to 0.125
- w_out: bfloat16 [8, 6144, 2048], P('expert', 'mp'), may hold values from -0.078125 to 0.078125
Outputs:
- mixed: bfloat16 [2, 2560, 2048], P(None, 'expert', 'mp')
Inputs may be any that keep to these rules, and one draw needn't show every extreme that they name: `slot_index`: within one aligned block of 320 tokens of a group, no two kept tokens share both expert and slot; in every group some expert has all 6 slots of every block taken. Dropped tokens carry a slot value too, which means nothing.
All inputs are finite; a program needn't handle non-finite values.
Results may differ from a plain program's by a relative error of at most 0.018.
Values may be sent and summed in bfloat16 or wider, within the bound.
A program may use at most 64 MiB of HBM per device.

v0:
```python
import jax
import jax.numpy as jnp
from jax import lax
from jax.sharding import PartitionSpec as P

GROUPS = 2
CAP = 6


def slot_table(expert_index, slot_index, kept_mask, experts):
    code = jnp.where(kept_mask > 0, expert_index * CAP + slot_index, -1)
    places = lax.broadcasted_iota(jnp.int32, (experts * CAP, code.shape[0]), 0)
    return (places == code[None, :]).astype(jnp.bfloat16)


def expert_pass(received, w_first, w_second, gather_rows, scatter_sums, send_back):
    source, slots, narrow = received.shape
    flat = received.reshape(source * slots, narrow)
    hidden_width = w_first.shape[1]

    def add_piece(total, piece, start):
        return jnp.dot(piece, w_first, preferred_element_type=jnp.float32)

    pre = gather_rows(flat, add_piece, jnp.zeros((source * slots, hidden_width), jnp.float32))
    hidden = jnp.maximum(pre, 0.0).astype(jnp.bfloat16)
    whole = jnp.dot(hidden, w_second, preferred_element_type=jnp.float32)
    summed = scatter_sums(whole)
    outgoing = summed.astype(jnp.bfloat16).reshape(source, slots, narrow)
    return send_back(outgoing)


def combine(table, returned, gate):
    flat = returned.reshape(returned.shape[0] * returned.shape[1], returned.shape[2])
    picked = lax.dot_general(
        table, flat, (((0,), (0,)), ((), ())), preferred_element_type=jnp.float32
    )
    return (gate[:, None] * picked).astype(jnp.bfloat16)


def on_device(tokens, expert_index, slot_index, kept_mask, gate_prob, w_in, w_out):
    experts = lax.axis_size("expert")
    w_first = w_in[0]
    w_second = w_out[0]
    narrow = tokens.shape[2]
    tables = []
    outgoing = []
    for group in range(GROUPS):
        table = slot_table(expert_index[group], slot_index[group], kept_mask[group], experts)
        tables.append(table)
        packed = jnp.dot(table, tokens[group], preferred_element_type=jnp.float32).astype(
            jnp.bfloat16
        )
        outgoing.append(packed.reshape(experts, CAP, narrow))
    results = []
    stacked = jnp.concatenate(outgoing, axis=1)
    returned = expert_pass(
        lax.all_to_all(stacked, "expert", split_axis=0, concat_axis=0, tiled=True),
        w_first,
        w_second,
        lambda flat, fold, start_value: fold(
            start_value, lax.all_gather(flat, "mp", axis=1, tiled=True), jnp.int32(0)
        ),
        lambda whole: lax.psum_scatter(
            whole.astype(jnp.bfloat16), "mp", scatter_dimension=1, tiled=True
        ).astype(jnp.float32),
        lambda outbound: lax.all_to_all(
            outbound, "expert", split_axis=0, concat_axis=0, tiled=True
        ),
    )
    for group in range(GROUPS):
        own = returned[:, group * CAP : (group + 1) * CAP, :]
        results.append(combine(tables[group], own, gate_prob[group]))
    return jnp.stack(results)


def solution(mesh):
    placed = (
        P(None, "expert", "mp"),
        P(None, "expert"),
        P(None, "expert"),
        P(None, "expert"),
        P(None, "expert"),
        P("expert", None, "mp"),
        P("expert", "mp", None),
    )
    return jax.shard_map(
        on_device, mesh=mesh, in_specs=placed, out_specs=P(None, "expert", "mp"), check_vma=False
    )
```

profile of v0, /device:TPU:0, one launch (start us, length us, event | category | flops | bytes accessed | tf_op | source)
XLA Modules:
  0.0 84.2 jit_solution(15073820139488619911)
XLA Ops:
  6.5 0.0 reduce-scatter.2.cloned.1.call-start
  6.5 0.8 fusion.28
  7.3 1.1 %convolution_convert_fusion.1 = bf16[48,512]{1,0:T(8,128)(2,1)S(1)} fusion(bf16[2,320,512]{2,1,0:T(8,128)(2,1)} %param.7, s32[320]{0:T(512)S(1)} %get-tuple-element.5), kind=kOutput, calls=%fused_computation.14 | convolution fusion | flops 15768576 | bytes 378112 | tf_op jit(solution)/shard_map/dot_general | solution.py:50
  8.5 1.1 %convolution_convert_fusion = bf16[48,512]{1,0:T(8,128)(2,1)S(1)} fusion(bf16[2,320,512]{2,1,0:T(8,128)(2,1)} %param.7, s32[320]{0:T(512)S(1)} %get-tuple-element.6), kind=kOutput, calls=%fused_computation.13 | convolution fusion | flops 15768576 | bytes 378112 | tf_op jit(solution)/shard_map/dot_general | solution.py:50
  9.7 12.9 %all_to_all.10 = bf16[8,12,512]{2,1,0:T(8,128)(2,1)S(1)} all-to-all(bf16[8,12,512]{2,1,0:T(8,128)(2,1)S(1)} %pad_maximum_fusion.1), channel_id=1, replica_groups=mesh['expert'=8,'mp'=4] {'expert'}, dimensions={0} | all-to-all | bytes 196608 | tf_op jit(solution)/shard_map/all_to_all | solution.py:57
  22.7 9.5 %all_gather.3 = bf16[96,2048]{1,0:T(8,128)(2,1)S(1)} all-gather(bf16[96,512]{1,0:T(8,128)(2,1)S(1)} %reshape.22), channel_id=1, replica_groups=mesh['expert'=8,'mp'=4] {'mp'}, dimensions={1}, use_global_device_ids=true | all-gather | bytes 491520 | tf_op jit(solution)/shard_map/all_gather | solution.py:61
  32.2 0.0 copy-start
  32.2 7.5 %fusion.7 = bf16[96,2048]{1,0:T(8,128)(2,1)} fusion(bf16[1,1536,2048]{2,1,0:T(8,128)(2,1)} %param.13, bf16[96,2048]{1,0:T(8,128)(2,1)S(1)} %all_gather.3, bf16[1,2048,1536]{2,1,0:T(8,128)(2,1)} %param.12), kind=kOutput, calls=%fused_computation.5 | convolution fusion | flops 1208451072 | bytes 13369344 | tf_op jit(solution)/shard_map/dot_general | solution.py:26
  39.7 0.0 reduce-scatter.2.cloned.1.call-update
  39.7 23.1 %reduce-scatter.2.cloned.1.call-done = bf16[96,512]{1,0:T(8,128)(2,1)} async-done(((bf16[96,2048]{1,0:T(8,128)(2,1)}), bf16[96,512]{1,0:T(8,128)(2,1)}) %reduce-scatter.2.cloned.1.call-update) | async-done | bytes 98320 | tf_op jit(solution)/shard_map/reduce_scatter | solution.py:63
  62.8 1.6 %reshape.23 = bf16[8,12,512]{2,1,0:T(8,128)(2,1)} reshape(bf16[96,512]{1,0:T(8,128)(2,1)} %reduce-scatter.2.cloned.1.call-done) | data formatting | bytes 196608 | tf_op jit(solution)/shard_map/reshape | solution.py:28
  64.4 4.6 %all-to-all-start.1 = ((bf16[8,12,512]{2,1,0:T(8,128)(2,1)}), bf16[8,12,512]{2,1,0:T(8,128)(2,1)S(1)}, u32[]{:S(2)}, u32[]{:S(2)}) async-start(bf16[8,12,512]{2,1,0:T(8,128)(2,1)} %reshape.23), calls=%async_computation.2 | async-start | bytes 262144 | tf_op jit(solution)/shard_map/all_to_all | solution.py:66
  69.0 0.0 copy-done
  69.0 6.7 %all-to-all-done.1 = bf16[8,12,512]{2,1,0:T(8,128)(2,1)S(1)} async-done(((bf16[8,12,512]{2,1,0:T(8,128)(2,1)}), bf16[8,12,512]{2,1,0:T(8,128)(2,1)S(1)}, u32[]{:S(2)}, u32[]{:S(2)}) %all-to-all-start.1) | async-done | bytes 98336 | tf_op jit(solution)/shard_map/all_to_all | solution.py:66
  75.9 0.3 fusion.15
  76.2 0.3 fusion.16
  76.5 0.9 %pad_maximum_fusion = bf16[2,320,512]{2,1,0:T(8,128)(2,1)} fusion(bf16[1,320,512]{2,1,0:T(8,128)(2,1)S(1)} %fusion.15, bf16[1,320,512]{2,1,0:T(8,128)(2,1)S(1)} %fusion.16), kind=kLoop, calls=%fused_computation.15 | loop fusion | flops 327680 | bytes 1310720 | tf_op jit(solution)/shard_map/stack | solution.py:73
  (8 shorter events, 0.2 us)
Async XLA Ops:
  6.5 56.3 %reduce-scatter.2.cloned.1.call-start = ((), (), s32[]{:S(2)}) async-start(), calls=%async_computation.3 | async-start | bytes 491520 | tf_op jit(solution)/shard_map/reduce_scatter | solution.py:63
  32.2 36.8 %copy-start = (f32[2,320]{1,0:T(2,128)S(1)}, f32[2,320]{1,0:T(2,128)}, u32[]{:S(2)}) copy-start(f32[2,320]{1,0:T(2,128)} %param.11) | copy-start | bytes 7684
  64.4 11.3 %all-to-all-start.1 = ((bf16[8,12,512]{2,1,0:T(8,128)(2,1)}), bf16[8,12,512]{2,1,0:T(8,128)(2,1)S(1)}, u32[]{:S(2)}, u32[]{:S(2)}) async-start(bf16[8,12,512]{2,1,0:T(8,128)(2,1)} %reshape.23), calls=%async_computation.2 | async-start | bytes 262144 | tf_op jit(solution)/shard_map/all_to_all | solution.py:66
Sparse Core Ops, SparseCore 0:
  39.8 22.9 reduce-scatter.1
where the time goes:
time: 84.6 us; the launch traced here: 84.2 us
  waiting for transfers between devices  29.9 us (35%)
  blocking collectives  22.4 us (26%)
  between operations  13.5 us (16%)
  matrix products  10.4 us (12%)
  starting transfers between devices  4.6 us (5%)
  local copies, waits for them, and re-layouts  1.75 us (2%)
  other arithmetic  1.73 us (2%)
    reduce_scatter x1, waiting for transfers between devices, on_device(): lax.psum_scatter(whole.astype(jnp.bfloat16), 'mp', scatter_dimension=1, t...  23.1 us
    all_to_all x1, blocking collectives, on_device(): lax.all_to_all(stacked, 'expert', split_axis=0, concat_axis=0, tiled=True)  12.9 us
    all_gather x1, blocking collectives, on_device(): lax.all_gather(flat, 'mp', axis=1, tiled=True)  9.52 us
    dot_general x1, matrix products, expert_pass(): whole = jnp.dot(hidden, w_second, preferred_element_type=jnp.float32)  7.49 us
    all_to_all x1, waiting for transfers between devices, on_device(): lax.all_to_all(outbound, 'expert', split_axis=0, concat_axis=0, tiled=True)  6.72 us
    all_to_all x1, starting transfers between devices, on_device(): lax.all_to_all(outbound, 'expert', split_axis=0, concat_axis=0, tiled=True)  4.59 us
    dot_general x2, matrix products, on_device(): jnp.dot(table, tokens[group], preferred_element_type=jnp.float32)  2.28 us
  transfers between devices with their start and end apart: 2, of which 2 were waited for; matrix products, arithmetic and copies ran while one was open for 0% of the time, Pallas kernels for 0%

commit v1 on v0

--- a/solution.py
+++ b/solution.py
@@ -58,7 +58,7 @@
         w_first,
         w_second,
         lambda flat, fold, start_value: fold(
-            start_value, lax.all_gather(flat, "mp", axis=1, tiled=True), jnp.int32(0)
+            start_value, jnp.concatenate(lax.all_gather(flat, "mp"), axis=1), jnp.int32(0)
         ),
         lambda whole: lax.psum_scatter(
             whole.astype(jnp.bfloat16), "mp", scatter_dimension=1, tiled=True

time: 84.6 us -> 84.6 us (level)
  no operation moved by 1% of the time
where the time goes in v1:
time: 84.6 us; the launch traced here: 84.2 us
  waiting for transfers between devices  29.9 us (35%)
  blocking collectives  22.4 us (26%)
  between operations  13.5 us (16%)
  matrix products  10.4 us (12%)
  starting transfers between devices  4.6 us (5%)
  local copies, waits for them, and re-layouts  1.78 us (2%)
  other arithmetic  1.73 us (2%)
    reduce_scatter x1, waiting for transfers between devices, on_device(): lax.psum_scatter(whole.astype(jnp.bfloat16), 'mp', scatter_dimension=1, t...  23.1 us
    all_to_all x1, blocking collectives, on_device(): lax.all_to_all(stacked, 'expert', split_axis=0, concat_axis=0, tiled=True)  12.9 us
    all_gather x1, blocking collectives, on_device(): lax.all_gather(flat, 'mp')  9.52 us
    dot_general x1, matrix products, expert_pass(): whole = jnp.dot(hidden, w_second, preferred_element_type=jnp.float32)  7.49 us
    all_to_all x1, waiting for transfers between devices, on_device(): lax.all_to_all(outbound, 'expert', split_axis=0, concat_axis=0, tiled=True)  6.72 us
    all_to_all x1, starting transfers between devices, on_device(): lax.all_to_all(outbound, 'expert', split_axis=0, concat_axis=0, tiled=True)  4.59 us
    dot_general x2, matrix products, on_device(): jnp.dot(table, tokens[group], preferred_element_type=jnp.float32)  2.28 us
  transfers between devices with their start and end apart: 2, of which 2 were waited for; matrix products, arithmetic and copies ran while one was open for 0% of the time, Pallas kernels for 0%

profile of v1, /device:TPU:0, one launch (start us, length us, event | category | flops | bytes accessed | tf_op | source)
XLA Modules:
  0.0 84.2 jit_solution(8524384125262805436)
XLA Ops:
  6.5 0.0 reduce-scatter.2.cloned.1.call-start
  6.5 0.8 fusion.28
  7.3 1.1 %convolution_convert_fusion.1 = bf16[48,512]{1,0:T(8,128)(2,1)S(1)} fusion(bf16[2,320,512]{2,1,0:T(8,128)(2,1)} %param.7, s32[320]{0:T(512)S(1)} %get-tuple-element.5), kind=kOutput, calls=%fused_computation.14 | convolution fusion | flops 15768576 | bytes 378112 | tf_op jit(solution)/shard_map/dot_general | solution.py:50
  8.5 1.1 %convolution_convert_fusion = bf16[48,512]{1,0:T(8,128)(2,1)S(1)} fusion(bf16[2,320,512]{2,1,0:T(8,128)(2,1)} %param.7, s32[320]{0:T(512)S(1)} %get-tuple-element.6), kind=kOutput, calls=%fused_computation.13 | convolution fusion | flops 15768576 | bytes 378112 | tf_op jit(solution)/shard_map/dot_general | solution.py:50
  9.7 12.9 %all_to_all.10 = bf16[8,12,512]{2,1,0:T(8,128)(2,1)S(1)} all-to-all(bf16[8,12,512]{2,1,0:T(8,128)(2,1)S(1)} %pad_maximum_fusion.1), channel_id=1, replica_groups=mesh['expert'=8,'mp'=4] {'expert'}, dimensions={0} | all-to-all | bytes 196608 | tf_op jit(solution)/shard_map/all_to_all | solution.py:57
  22.7 9.5 %all_gather.3 = bf16[4,96,512]{2,1,0:T(8,128)(2,1)S(1)} all-gather(bf16[1,96,512]{2,1,0:T(8,128)(2,1)S(1)} %all_gather_reshape.3), channel_id=1, replica_groups=mesh['expert'=8,'mp'=4] {'mp'}, dimensions={0}, use_global_device_ids=true | all-gather | bytes 491520 | tf_op jit(solution)/shard_map/all_gather | solution.py:61
  32.2 0.0 copy-start
  32.2 7.5 %fusion.7 = bf16[96,2048]{1,0:T(8,128)(2,1)} fusion(bf16[1,1536,2048]{2,1,0:T(8,128)(2,1)} %param.13, bf16[96,2048]{1,0:T(8,128)(2,1)S(1)} %bitcast.30, bf16[1,2048,1536]{2,1,0:T(8,128)(2,1)} %param.12), kind=kOutput, calls=%fused_computation.5 | convolution fusion | flops 1208451072 | bytes 13369344 | tf_op jit(solution)/shard_map/dot_general | solution.py:26
  39.7 0.0 reduce-scatter.2.cloned.1.call-update
  39.8 23.1 %reduce-scatter.2.cloned.1.call-done = bf16[96,512]{1,0:T(8,128)(2,1)} async-done(((bf16[96,2048]{1,0:T(8,128)(2,1)}), bf16[96,512]{1,0:T(8,128)(2,1)}) %reduce-scatter.2.cloned.1.call-update) | async-done | bytes 98320 | tf_op jit(solution)/shard_map/reduce_scatter | solution.py:63
  62.9 1.6 %reshape.27 = bf16[8,12,512]{2,1,0:T(8,128)(2,1)} reshape(bf16[96,512]{1,0:T(8,128)(2,1)} %reduce-scatter.2.cloned.1.call-done) | data formatting | bytes 196608 | tf_op jit(solution)/shard_map/reshape | solution.py:28
  64.5 4.6 %all-to-all-start.1 = ((bf16[8,12,512]{2,1,0:T(8,128)(2,1)}), bf16[8,12,512]{2,1,0:T(8,128)(2,1)S(1)}, u32[]{:S(2)}, u32[]{:S(2)}) async-start(bf16[8,12,512]{2,1,0:T(8,128)(2,1)} %reshape.27), calls=%async_computation.2 | async-start | bytes 262144 | tf_op jit(solution)/shard_map/all_to_all | solution.py:66
  69.1 0.0 copy-done
  69.1 6.7 %all-to-all-done.1 = bf16[8,12,512]{2,1,0:T(8,128)(2,1)S(1)} async-done(((bf16[8,12,512]{2,1,0:T(8,128)(2,1)}), bf16[8,12,512]{2,1,0:T(8,128)(2,1)S(1)}, u32[]{:S(2)}, u32[]{:S(2)}) %all-to-all-start.1) | async-done | bytes 98336 | tf_op jit(solution)/shard_map/all_to_all | solution.py:66
  75.9 0.3 fusion.15
  76.2 0.3 fusion.16
  76.5 0.9 %pad_maximum_fusion = bf16[2,320,512]{2,1,0:T(8,128)(2,1)} fusion(bf16[1,320,512]{2,1,0:T(8,128)(2,1)S(1)} %fusion.15, bf16[1,320,512]{2,1,0:T(8,128)(2,1)S(1)} %fusion.16), kind=kLoop, calls=%fused_computation.15 | loop fusion | flops 327680 | bytes 1310720 | tf_op jit(solution)/shard_map/stack | solution.py:73
  (9 shorter events, 0.3 us)
Async XLA Ops:
  6.5 56.4 %reduce-scatter.2.cloned.1.call-start = ((), (), s32[]{:S(2)}) async-start(), calls=%async_computation.3 | async-start | bytes 491520 | tf_op jit(solution)/shard_map/reduce_scatter | solution.py:63
  32.2 36.8 %copy-start = (f32[2,320]{1,0:T(2,128)S(1)}, f32[2,320]{1,0:T(2,128)}, u32[]{:S(2)}) copy-start(f32[2,320]{1,0:T(2,128)} %param.11) | copy-start | bytes 7684
  64.5 11.3 %all-to-all-start.1 = ((bf16[8,12,512]{2,1,0:T(8,128)(2,1)}), bf16[8,12,512]{2,1,0:T(8,128)(2,1)S(1)}, u32[]{:S(2)}, u32[]{:S(2)}) async-start(bf16[8,12,512]{2,1,0:T(8,128)(2,1)} %reshape.27), calls=%async_computation.2 | async-start | bytes 262144 | tf_op jit(solution)/shard_map/all_to_all | solution.py:66
Sparse Core Ops, SparseCore 0:
  39.9 22.9 reduce-scatter.1
